TPU v7x, 32 devices: a whole 2x2x4 slice. The times are simulated.
32 devices in a mesh: gx: 4 (over y, x), gy: 2 (over core), gz: 4 (over z).
Axes of the slice: x: 2, y: 2, z: 4, core: 2. Of those that a mesh axis runs over, the one named last changes fastest.
Arguments:
- potential: float32 [240, 120, 512], P('gx', 'gy', 'gz'), may hold values from -6 to 6
- frag_root: int32 [3, 128], P(None, ('gx', 'gy', 'gz')), may hold values from 0 to 511, as said below
Outputs:
- frag_fields: float32 [128, 110592], P(('gx', 'gy', 'gz'))
Inputs may be any that keep to these rules, and one draw needn't show every extreme that they name: `frag_root`: fragment f is held by the device of linear index f // 4 (gx slowest). Along each dimension the box's first cell is the start of a block plus an offset in [-34, B - 34), B being that dimension's cells of one device. Along y and z that block is the holding device's own; along x it is the block of some device with the same gy and gz index, the anchor. Every anchor of a device supplies exactly 1 of its fragments.
All inputs are finite; a program needn't handle non-finite values.
Results may differ from a plain program's by a relative error of at most 0.00007.
Values sent between devices are 32-bit elements; how exact they have to be, the bound alone decides.
A program may use at most 320 MiB of HBM per device.

v0:
```python
import math

import jax
import jax.numpy as jnp
from jax import lax
from jax.experimental import pallas as pl
from jax.experimental.pallas import tpu as pltpu
from jax.sharding import PartitionSpec as P

G = 48
BOX = 68
HALO = 34
HIGH = lax.Precision.HIGH


def shift(array, axis, step):
    devices = lax.axis_size(axis)
    return lax.ppermute(array, axis, [(i, (i + step) % devices) for i in range(devices)])


def placed(start, cells, period, valid):
    place = cells - start[..., None]
    if period:
        place = jnp.mod(place, period)
    inside = jnp.logical_and(place >= 0, place < BOX)
    inside = jnp.logical_and(inside, valid[..., None])
    base = interp_values()
    index = jnp.where(inside, place, BOX)
    hot = (index[..., None, :] == jnp.arange(BOX, dtype=jnp.int32)[:, None]).astype(jnp.float32)
    return jnp.einsum("ax,...xe->...ae", base, hot, precision=lax.Precision.HIGHEST)


def interp_values():
    row_index = jnp.arange(G, dtype=jnp.int32)[:, None]
    col_index = jnp.arange(BOX, dtype=jnp.int32)[None, :]
    offset = row_index * BOX - col_index * G
    period = G * BOX
    summed = jnp.ones((G, BOX), jnp.float32)
    for harmonic in range(1, G // 2):
        phase_angle = jnp.mod(harmonic * offset, period).astype(jnp.float32)
        summed = summed + 2.0 * jnp.cos(2.0 * math.pi / period * phase_angle)
    return summed / BOX


LANES = 128
FOLD = LANES // HALO
STEPS = 4
BF = jnp.bfloat16
F32 = jnp.float32
FAR = -(1 << 20)


def split(value):
    high = value.astype(BF)
    return high, (value - high.astype(F32)).astype(BF)


def pack_kernel(pot, low, high):
    rows, by = pot.shape[1], pot.shape[2]
    lane = lax.broadcasted_iota(jnp.int32, (rows * by, LANES), 1)
    down = jnp.zeros((rows * by, LANES), F32)
    up = down
    for g in range(FOLD):
        v = pot[g].reshape(rows * by, LANES)
        mine = jnp.logical_and(lane >= g * HALO, lane < (g + 1) * HALO)
        down = jnp.where(mine, pltpu.roll(v, ((g + 1) * HALO) % LANES, 1), down)
        up = jnp.where(mine, pltpu.roll(v, g * HALO, 1) if g else v, up)
    low[...] = down.reshape(rows, by, LANES)
    high[...] = up.reshape(rows, by, LANES)


def pack(pot):
    fold, rows, by, bz = pot.shape
    step = rows // STEPS
    spec = pl.BlockSpec((step, by, LANES), lambda i: (i, 0, 0))
    shape = jax.ShapeDtypeStruct((rows, by, LANES), F32)
    return pl.pallas_call(
        pack_kernel,
        grid=(STEPS,),
        in_specs=[pl.BlockSpec((fold, step, by, LANES), lambda i: (0, i, 0, 0))],
        out_specs=[spec, spec],
        out_shape=[shape, shape],
        cost_estimate=pl.CostEstimate(flops=0, bytes_accessed=4 * pot.size * 2, transcendentals=0),
        name="pack_halos",
    )(pot)


def slab_kernel(ny, *refs):
    owns, lows, highs, out = refs[:ny], refs[ny:2 * ny], refs[2 * ny:3 * ny], refs[3 * ny]
    rows, by = owns[0].shape[1], owns[0].shape[2]
    pad = out.shape[2] // (2 * ny)
    half = ny * pad
    lane = lax.broadcasted_iota(jnp.int32, (pad, LANES), 1)
    blank = jnp.zeros((pad - by, LANES), F32)

    def full(v):
        return jnp.concatenate([v, blank], axis=0)

    for c in range(ny):
        for r in range(rows):
            up = full(highs[c][r])
            down = full(lows[c][r])
            for g in range(FOLD):
                first = full(owns[c][g, r])
                a = pltpu.roll(up, (-g * HALO) % LANES, 1) if g else up
                b = pltpu.roll(down, (HALO - g * HALO) % LANES, 1) if g != 1 else down
                second = jnp.where(lane < HALO, a, jnp.where(lane < 2 * HALO, b, 0.0))
                for side, v in ((0, first), (1, second)):
                    h, l = split(v)
                    cols = slice(side * LANES, (side + 1) * LANES)
                    out[g, r, c * pad:(c + 1) * pad, cols] = h
                    out[g, r, half + c * pad:half + (c + 1) * pad, cols] = l


def slabs(owns, lows, highs):
    ny = len(owns)
    fold, rows, by, bz = owns[0].shape
    pad = -(-by // 16) * 16
    step = rows // STEPS
    big = pl.BlockSpec((fold, step, by, LANES), lambda i: (0, i, 0, 0))
    small = pl.BlockSpec((step, by, LANES), lambda i: (i, 0, 0))
    return pl.pallas_call(
        lambda *refs: slab_kernel(ny, *refs),
        grid=(STEPS,),
        in_specs=[big] * ny + [small] * (2 * ny),
        out_specs=pl.BlockSpec((fold, step, 2 * ny * pad, 2 * LANES), lambda i: (0, i, 0, 0)),
        out_shape=jax.ShapeDtypeStruct((fold, rows, 2 * ny * pad, 2 * LANES), BF),
        cost_estimate=pl.CostEstimate(flops=0, bytes_accessed=16 * 1024 * 1024, transcendentals=0),
        name="build_slabs",
    )(*owns, *lows, *highs)


def contract_kernel(bx, yb, my, mz, out, lhs, wz, us):
    k = my.shape[2]
    for p in range(3):
        h, l = split(my[p])
        lhs[p, :G, :k] = h
        lhs[p, :G, k:] = h
        lhs[p, G:, :k] = l
        lhs[p, G:, k:] = jnp.zeros_like(l)
        h, l = split(mz[p])
        wz[p, 0] = h
        wz[p, 1] = l
    nl, nm = HALO // 8, bx // 8

    def row(p, x, s):
        r = jnp.dot(lhs[p], yb[x], preferred_element_type=F32)
        us[:, s, :] = r[:G] + r[G:]

    def finish(p):
        h, l = split(us[...].reshape(G * 8, us.shape[2]))
        dot = lambda a, b: jnp.dot(a, b, preferred_element_type=F32)
        return dot(h, wz[p, 0]) + dot(h, wz[p, 1]) + dot(l, wz[p, 0])

    def store(r, row0):
        for b in range(G):
            out[pl.ds(row0, 8), b * G:(b + 1) * G] = r[8 * b:8 * b + 8]

    def block(i, carry):
        p = (i >= nl).astype(jnp.int32) + (i >= nl + nm).astype(jnp.int32)
        x0 = jnp.where(p == 0, bx - HALO + 8 * i, jnp.where(p == 1, 8 * (i - nl), 8 * (i - nl - nm)))
        for s in range(8):
            row(p, x0 + s, s)
        store(finish(p), pl.multiple_of(8 * i, 8))
        return carry

    blocks = 2 * nl + nm
    lax.fori_loop(0, blocks, block, 0)
    tail = tail_rows(bx)
    for s, (p, x) in enumerate(tail):
        row(p, x, s)
    sub = lax.broadcasted_iota(jnp.int32, (G * 8, G), 0) % 8
    total = jnp.zeros((G * 8, G), F32)
    for p in range(3):
        places = [s for s, t in enumerate(tail) if t[0] == p]
        mine = jnp.logical_and(sub >= places[0], sub <= places[-1])
        total = jnp.where(mine, finish(p), total)
    store(total, 8 * blocks)


def tail_rows(bx):
    nl, nm = HALO // 8 * 8, bx // 8 * 8
    rows = [(0, bx - HALO + x) for x in range(nl, HALO)]
    rows += [(1, x) for x in range(nm, bx)]
    rows += [(2, x) for x in range(nl, HALO)]
    assert len(rows) == 8
    return rows


def row_order(bx):
    nl, nm = HALO // 8 * 8, bx // 8 * 8
    rows = [(0, bx - HALO + x) for x in range(nl)] + [(1, x) for x in range(nm)]
    return rows + [(2, x) for x in range(nl)] + tail_rows(bx)


def contract(bx, yb, my, mz):
    rows = len(row_order(bx))
    k = my.shape[2]
    width = yb.shape[2]
    return pl.pallas_call(
        lambda *refs: contract_kernel(bx, *refs),
        in_specs=[pl.BlockSpec(memory_space=pltpu.VMEM)] * 3,
        out_specs=pl.BlockSpec(memory_space=pltpu.VMEM),
        out_shape=jax.ShapeDtypeStruct((rows, G * G), F32),
        scratch_shapes=[
            pltpu.VMEM((3, 2 * G, 2 * k), BF),
            pltpu.VMEM((3, 2, width, G), BF),
            pltpu.VMEM((G, 8, width), F32),
        ],
        compiler_params=pltpu.CompilerParams(vmem_limit_bytes=40 * 1024 * 1024),
        cost_estimate=pl.CostEstimate(
            flops=6 * 10 ** 9, bytes_accessed=2 * yb.size + 4 * rows * G * G, transcendentals=0),
        name="contract_yz",
    )(yb, my, mz)


def body(potential, frag_root):
    bx, by, bz = potential.shape
    n = lax.axis_size("gx")
    ny = lax.axis_size("gy")
    nz = lax.axis_size("gz")
    ix, iy, iz = lax.axis_index("gx"), lax.axis_index("gy"), lax.axis_index("gz")
    total_x, total_y, total_z = bx * n, by * ny, bz * nz
    slots = frag_root.shape[1]

    folded = potential.reshape(FOLD, bx // FOLD, by, bz)
    low, high = pack(folded)
    low = shift(low, "gz", 1)
    high = shift(high, "gz", -1)
    owns = [folded] + [shift(folded, "gy", -j) for j in range(1, ny)]
    lows = [low] + [shift(low, "gy", -j) for j in range(1, ny)]
    highs = [high] + [shift(high, "gy", -j) for j in range(1, ny)]
    root = jnp.stack([frag_root] + [shift(frag_root, "gx", j) for j in range(1, n)])
    yb = slabs(owns, lows, highs)
    yb = yb.reshape(bx, yb.shape[2], yb.shape[3])

    anchor = jnp.mod(root[:, 0] + HALO, total_x) // bx
    start_y = jnp.mod(root[:, 1] - iy * by, total_y)
    start_z = jnp.mod(root[:, 2] + HALO - iz * bz, total_z)
    pad = -(-by // 16) * 16
    e = jnp.arange(ny * pad, dtype=jnp.int32)
    cells_y = e // pad * by + e % pad
    real_y = e % pad < by
    e = jnp.arange(2 * LANES, dtype=jnp.int32)
    cells_z = jnp.where(e < bz + HALO, e + HALO, jnp.where(e < bz + 2 * HALO, e - bz - HALO, FAR))
    delta = jnp.array([1, 0, -1], jnp.int32)
    hit = anchor[:, None, :] == jnp.mod(ix + delta, n)[None, :, None]
    valid = jnp.any(hit, axis=2)
    pick = lambda v: jnp.sum(jnp.where(hit, v[:, None, :], 0), axis=2)
    my = placed(pick(start_y), cells_y, total_y, valid)
    my = jnp.where(real_y, my, 0.0)
    mz = placed(pick(start_z), cells_z, None, valid).transpose(0, 1, 3, 2)

    order = [j for j in range(2, n, 2)] + [j for j in range(n) if j % 2]
    got = [None] * n
    for j in order:
        got[j] = shift(contract(bx, yb, my[j], mz[j]), "gx", -j)
    got[0] = contract(bx, yb, my[0], mz[0])

    mine = jnp.mod(frag_root[0] + HALO, total_x)
    slab = mine // bx
    rel = mine - slab * bx
    rows = row_order(bx)
    part = jnp.array([p for p, x in rows], jnp.int32)
    ext = jnp.array([x - (bx - HALO) if p == 0 else x + HALO + (p - 1) * bx for p, x in rows], jnp.int32)
    mx = placed(rel, ext, None, jnp.ones((slots,), bool))
    source = jnp.mod(slab[:, None] - ix + part[None, :] - 1, n)
    fields = None
    for j in [0] + order:
        m = jnp.where((source == j)[:, None, :], mx, 0.0).reshape(slots * G, -1)
        term = jnp.dot(m, got[j], precision=HIGH)
        fields = term if fields is None else fields + term
    return fields.reshape(slots, -1)


def solution(mesh):
    return jax.shard_map(
        body,
        mesh=mesh,
        in_specs=(P("gx", "gy", "gz"), P(None, ("gx", "gy", "gz"))),
        out_specs=P(("gx", "gy", "gz"), None),
        check_vma=False,
    )
```

profile of v0, /device:TPU:0, one launch (start us, length us, event | category | flops | bytes accessed | tf_op | source)
XLA Modules:
  0.0 138.0 jit_solution(849155628178688133)
XLA Ops:
  0.0 3.0 %collective-permute-start.5 = (s32[3,4]{1,0:T(4,128)}, s32[3,4]{1,0:T(4,128)S(1)}, u32[]{:S(2)}, u32[]{:S(2)}) collective-permute-start(s32[3,4]{1,0:T(4,128)} %param.6), channel_id=1, source_target_pairs={{0,8},{8,16},{16,24},{24,0},{1,9},{9,17},{17,25},{25,1},{2,10},{10... | collective-permute-start | bytes 152 | tf_op jit(solution)/shard_map/ppermute | solution.py:18
  3.0 1.0 collective-permute-start.7
  4.1 1.9 %collective-permute-start.6 = (s32[3,4]{1,0:T(4,128)}, s32[3,4]{1,0:T(4,128)S(1)}, u32[]{:S(2)}, u32[]{:S(2)}) collective-permute-start(s32[3,4]{1,0:T(4,128)} %param.6), channel_id=1, source_target_pairs={{0,16},{8,24},{16,0},{24,8},{1,17},{9,25},{17,1},{25,9},{2,18},{10... | collective-permute-start | bytes 152 | tf_op jit(solution)/shard_map/ppermute | solution.py:18
  6.0 0.0 collective-permute-start
  6.0 4.0 %pack_halos.1 = (f32[20,60,128]{2,1,0:T(8,128)}, f32[20,60,128]{2,1,0:T(8,128)}) custom-call(f32[3,20,60,128]{3,2,1,0:T(8,128)} %bitcast.67), custom_call_target="tpu_custom_call" | custom-call | bytes 3686400 | tf_op jit(solution)/shard_map/pack_halos/pallas_call | solution.py:77
  10.0 1.6 %collective-permute-start.1 = (f32[20,60,128]{2,1,0:T(8,128)}, f32[20,60,128]{2,1,0:T(8,128)S(1)}, u32[]{:S(2)}, u32[]{:S(2)}) collective-permute-start(f32[20,60,128]{2,1,0:T(8,128)} %get-tuple-element.7), channel_id=1, source_target_pairs={{0,1},{1,2},{2,3},{3,0},{4,5},{5,6},{6,7},{7,4},{8,9},{9,10},{10,1... | collective-permute-start | bytes 1843208 | tf_op jit(solution)/shard_map/ppermute | solution.py:18
  11.7 0.1 subtract_select_fusion.1
  11.7 0.1 broadcast_compare_fusion.3
  11.8 2.2 %fusion.124 = f32[48,68]{1,0:T(8,128)S(1)} fusion(s32[68]{0:T(128)S(1)} %iota_multiply_fusion, s32[48]{0:T(128)S(1)} %iota_multiply_fusion.1), kind=kLoop, calls=%fused_computation.188 | loop fusion | flops 829056 | bytes 13520 | tf_op jit(solution)/shard_map/div | solution.py:42
  14.1 0.0 collective-permute-done.5
  14.1 2.3 %collective-permute-start.3 = (f32[20,60,128]{2,1,0:T(8,128)}, f32[20,60,128]{2,1,0:T(8,128)S(1)}, u32[]{:S(2)}, u32[]{:S(2)}) collective-permute-start(f32[20,60,128]{2,1,0:T(8,128)} %get-tuple-element.8), channel_id=1, source_target_pairs={{0,3},{1,0},{2,1},{3,2},{4,7},{5,4},{6,5},{7,6},{8,11},{9,8},{10,9... | collective-permute-start | bytes 1843208 | tf_op jit(solution)/shard_map/ppermute | solution.py:18
  16.4 0.0 collective-permute-done.7
  16.4 0.0 collective-permute-done.6
  16.4 0.2 compare_reduce_fusion
  16.6 0.1 copy.11
  16.8 0.3 fusion.228
  17.0 0.1 copy.12
  17.1 0.1 copy.10
  17.2 0.1 and_select_fusion.1
  17.3 0.3 fusion.2
  17.6 12.0 %collective-permute-done.1.refs_2_ = f32[20,60,128]{2,1,0:T(8,128)S(1)} collective-permute-done((f32[20,60,128]{2,1,0:T(8,128)}, f32[20,60,128]{2,1,0:T(8,128)S(1)}, u32[]{:S(2)}, u32[]{:S(2)}) %collective-permute-start.1) | collective-permute-done | bytes 614432 | tf_op jit(solution)/shard_map/ppermute | solution.py:18
  29.6 0.0 collective-permute-start.2
  29.6 13.6 %collective-permute-done.3.refs_4_ = f32[20,60,128]{2,1,0:T(8,128)S(1)} collective-permute-done((f32[20,60,128]{2,1,0:T(8,128)}, f32[20,60,128]{2,1,0:T(8,128)S(1)}, u32[]{:S(2)}, u32[]{:S(2)}) %collective-permute-start.3) | collective-permute-done | bytes 614432 | tf_op jit(solution)/shard_map/ppermute | solution.py:18
  43.2 0.0 collective-permute-start.4
  43.3 0.1 subtract_select_fusion
  43.4 0.9 fusion.4
  44.3 0.1 slice_bitcast_fusion.3
  44.5 0.9 collective-permute-done.4.refs_5_
  45.3 0.8 copy-done.4
  46.2 0.0 collective-permute-done.refs_1_
  46.2 7.1 %build_slabs.1 = bf16[3,20,256,256]{3,2,1,0:T(8,128)(2,1)} custom-call(f32[3,20,60,128]{3,2,1,0:T(8,128)} %bitcast.68, f32[3,20,60,128]{3,2,1,0:T(8,128)} %collective-permute-done.refs_1_, f32[20,60,128]{2,1,0:T(8,128)} %copy-done.1, f32[20,60,128]{2,1,0:T(8,128)} %copy-done.3, f32[20,60,128]{2,1,0:T(8,128)} %copy-done.2, f32[20,60,128]{2,1,0:T(8,128)} %copy-done.4), custom_call_target="tpu_custom_call" | custom-call | bytes 16777216 | tf_op jit(solution)/shard_map/build_slabs/pallas_call | solution.py:122
  53.3 3.2 %copy-done = bf16[3,20,256,256]{3,2,1,0:T(8,128)(2,1)S(1)} copy-done((bf16[3,20,256,256]{3,2,1,0:T(8,128)(2,1)S(1)}, bf16[3,20,256,256]{3,2,1,0:T(8,128)(2,1)}, u32[]{:S(2)}) %copy-start) | copy-done | bytes 7864344
  56.5 11.3 %contract_yz.5 = f32[128,2304]{1,0:T(8,128)S(1)} custom-call(bf16[60,256,256]{2,1,0:T(8,128)(2,1)S(1)} %bitcast.62, f32[3,48,128]{2,1,0:T(8,128)S(1)} %get-tuple-element.21.refs_1_, f32[3,256,48]{2,1,0:T(8,128)S(1)} %get-tuple-element.16.refs_2_), custom_call_target="tpu_custom_call" | custom-call | flops 6000000000 | bytes 9043968 | tf_op jit(solution)/shard_map/contract_yz/pallas_call | solution.py:200
  67.8 0.6 collective-permute-start.8
  68.3 11.3 %contract_yz.6 = f32[128,2304]{1,0:T(8,128)S(1)} custom-call(bf16[60,256,256]{2,1,0:T(8,128)(2,1)S(1)} %bitcast.63, f32[3,48,128]{2,1,0:T(8,128)S(1)} %get-tuple-element.20.refs_1_, f32[3,256,48]{2,1,0:T(8,128)S(1)} %get-tuple-element.15.refs_2_), custom_call_target="tpu_custom_call" | custom-call | flops 6000000000 | bytes 9043968 | tf_op jit(solution)/shard_map/contract_yz/pallas_call | solution.py:200
  79.6 1.6 %collective-permute-start.9 = (f32[128,2304]{1,0:T(8,128)S(1)}, f32[128,2304]{1,0:T(8,128)S(1)}, u32[]{:S(2)}, u32[]{:S(2)}) collective-permute-start(f32[128,2304]{1,0:T(8,128)S(1)} %contract_yz.6), channel_id=1, source_target_pairs={{0,24},{8,0},{16,8},{24,16},{1,25},{9,1},{17,9},{25,17},{2,26},{10... | collective-permute-start | bytes 3538952 | tf_op jit(solution)/shard_map/ppermute | solution.py:18
  81.2 11.3 %contract_yz.7 = f32[128,2304]{1,0:T(8,128)S(1)} custom-call(bf16[60,256,256]{2,1,0:T(8,128)(2,1)S(1)} %bitcast.64, f32[3,48,128]{2,1,0:T(8,128)S(1)} %get-tuple-element.19.refs_1_, f32[3,256,48]{2,1,0:T(8,128)S(1)} %get-tuple-element.17.refs_2_), custom_call_target="tpu_custom_call" | custom-call | flops 6000000000 | bytes 9043968 | tf_op jit(solution)/shard_map/contract_yz/pallas_call | solution.py:200
  92.5 0.7 collective-permute-start.10
  93.2 0.2 broadcast_select_fusion.3
  93.4 11.3 %contract_yz.4 = f32[128,2304]{1,0:T(8,128)S(1)} custom-call(bf16[60,256,256]{2,1,0:T(8,128)(2,1)S(1)} %bitcast.65, f32[3,48,128]{2,1,0:T(8,128)S(1)} %get-tuple-element.18.refs_1_, f32[3,256,48]{2,1,0:T(8,128)S(1)} %get-tuple-element.14.refs_2_), custom_call_target="tpu_custom_call" | custom-call | flops 6000000000 | bytes 9043968 | tf_op jit(solution)/shard_map/contract_yz/pallas_call | solution.py:200
  104.7 0.0 collective-permute-done.8
  104.7 0.9 fusion.240
  105.6 2.9 %collective-permute-done.9 = f32[128,2304]{1,0:T(8,128)S(1)} collective-permute-done((f32[128,2304]{1,0:T(8,128)S(1)}, f32[128,2304]{1,0:T(8,128)S(1)}, u32[]{:S(2)}, u32[]{:S(2)}) %collective-permute-start.9) | collective-permute-done | bytes 1179680 | tf_op jit(solution)/shard_map/ppermute | solution.py:18
  108.5 0.9 fusion.241
  109.4 24.5 %collective-permute-done.10 = f32[128,2304]{1,0:T(8,128)S(1)} collective-permute-done((f32[128,2304]{1,0:T(8,128)S(1)}, f32[128,2304]{1,0:T(8,128)S(1)}, u32[]{:S(2)}, u32[]{:S(2)}) %collective-permute-start.10) | collective-permute-done | bytes 1179680 | tf_op jit(solution)/shard_map/ppermute | solution.py:18
  133.9 0.9 fusion.242
  134.8 1.1 fusion.1
  135.9 2.1 %reshape.249 = f32[4,110592]{1,0:T(4,128)} reshape(f32[192,2304]{1,0:T(8,128)S(1)} %fusion.1) | data formatting | bytes 3538944 | tf_op jit(solution)/shard_map/reshape | solution.py:273
  (27 shorter events, 0.2 us)
Async XLA Ops:
  0.0 11.6 %copy-start.8 = (s32[3]{0:T(128)S(1)}, s32[3]{0:T(128)}, u32[]{:S(2)}) copy-start(s32[3]{0:T(128)} %constant.436.clone) | copy-start | bytes 40
  0.0 11.7 %copy-start.7 = (s32[128]{0:T(128)S(1)}, s32[128]{0:T(128)}, u32[]{:S(2)}) copy-start(s32[128]{0:T(128)} %constant.438.clone) | copy-start | bytes 1540
  0.0 11.7 %copy-start.6 = (s32[128]{0:T(128)S(1)}, s32[128]{0:T(128)}, u32[]{:S(2)}) copy-start(s32[128]{0:T(128)} %constant.437.clone) | copy-start | bytes 1540
  0.0 11.6 %copy-start.5 = (s32[3,4]{1,0:T(4,128)S(1)}, s32[3,4]{1,0:T(4,128)}, u32[]{:S(2)}) copy-start(s32[3,4]{1,0:T(4,128)} %param.6) | copy-start | bytes 148
  0.0 14.1 %collective-permute-start.5 = (s32[3,4]{1,0:T(4,128)}, s32[3,4]{1,0:T(4,128)S(1)}, u32[]{:S(2)}, u32[]{:S(2)}) collective-permute-start(s32[3,4]{1,0:T(4,128)} %param.6), channel_id=1, source_target_pairs={{0,8},{8,16},{16,24},{24,0},{1,9},{9,17},{17,25},{25,1},{2,10},{10... | collective-permute-start | bytes 152 | tf_op jit(solution)/shard_map/ppermute | solution.py:18
  3.0 13.3 %collective-permute-start.7 = (s32[3,4]{1,0:T(4,128)}, s32[3,4]{1,0:T(4,128)S(1)}, u32[]{:S(2)}, u32[]{:S(2)}) collective-permute-start(s32[3,4]{1,0:T(4,128)} %param.6), channel_id=1, source_target_pairs={{0,24},{8,0},{16,8},{24,16},{1,25},{9,1},{17,9},{25,17},{2,26},{10... | collective-permute-start | bytes 152 | tf_op jit(solution)/shard_map/ppermute | solution.py:18
  4.1 12.3 %collective-permute-start.6 = (s32[3,4]{1,0:T(4,128)}, s32[3,4]{1,0:T(4,128)S(1)}, u32[]{:S(2)}, u32[]{:S(2)}) collective-permute-start(s32[3,4]{1,0:T(4,128)} %param.6), channel_id=1, source_target_pairs={{0,16},{8,24},{16,0},{24,8},{1,17},{9,25},{17,1},{25,9},{2,18},{10... | collective-permute-start | bytes 152 | tf_op jit(solution)/shard_map/ppermute | solution.py:18
  6.0 40.2 %collective-permute-start = (f32[3,20,60,128]{3,2,1,0:T(8,128)}, f32[3,20,60,128]{3,2,1,0:T(8,128)}, u32[]{:S(2)}, u32[]{:S(2)}) collective-permute-start(f32[3,20,60,128]{3,2,1,0:T(8,128)} %bitcast.66), channel_id=1, source_target_pairs={{0,4},{4,0},{1,5},{5,1},{2,6},{6,2},{3,7},{7,3},{8,12},{12,8},{9,1... | collective-permute-start | bytes 5529608 | tf_op jit(solution)/shard_map/ppermute | solution.py:18
  10.0 19.7 %collective-permute-start.1 = (f32[20,60,128]{2,1,0:T(8,128)}, f32[20,60,128]{2,1,0:T(8,128)S(1)}, u32[]{:S(2)}, u32[]{:S(2)}) collective-permute-start(f32[20,60,128]{2,1,0:T(8,128)} %get-tuple-element.7), channel_id=1, source_target_pairs={{0,1},{1,2},{2,3},{3,0},{4,5},{5,6},{6,7},{7,4},{8,9},{9,10},{10,1... | collective-permute-start | bytes 1843208 | tf_op jit(solution)/shard_map/ppermute | solution.py:18
  14.1 29.2 %collective-permute-start.3 = (f32[20,60,128]{2,1,0:T(8,128)}, f32[20,60,128]{2,1,0:T(8,128)S(1)}, u32[]{:S(2)}, u32[]{:S(2)}) collective-permute-start(f32[20,60,128]{2,1,0:T(8,128)} %get-tuple-element.8), channel_id=1, source_target_pairs={{0,3},{1,0},{2,1},{3,2},{4,7},{5,4},{6,5},{7,6},{8,11},{9,8},{10,9... | collective-permute-start | bytes 1843208 | tf_op jit(solution)/shard_map/ppermute | solution.py:18
  29.6 14.8 %copy-start.1 = (f32[20,60,128]{2,1,0:T(8,128)}, f32[20,60,128]{2,1,0:T(8,128)S(1)}, u32[]{:S(2)}) copy-start(f32[20,60,128]{2,1,0:T(8,128)S(1)} %collective-permute-done.1.refs_2_) | copy-start | bytes 1843204
  29.6 14.8 %collective-permute-start.2 = (f32[20,60,128]{2,1,0:T(8,128)S(1)}, f32[20,60,128]{2,1,0:T(8,128)S(1)}, u32[]{:S(2)}, u32[]{:S(2)}) collective-permute-start(f32[20,60,128]{2,1,0:T(8,128)S(1)} %collective-permute-done.1.refs_2_), channel_id=1, source_target_pairs={{0,4},{4,0},{1,5},{5,1},{2,6},{6,2},{3,7},{7,3},{8,12},{12,8},{9,1... | collective-permute-start | bytes 1843208 | tf_op jit(solution)/shard_map/ppermute | solution.py:18
  43.2 1.2 copy-start.2
  43.2 2.1 %collective-permute-start.4 = (f32[20,60,128]{2,1,0:T(8,128)S(1)}, f32[20,60,128]{2,1,0:T(8,128)S(1)}, u32[]{:S(2)}, u32[]{:S(2)}) collective-permute-start(f32[20,60,128]{2,1,0:T(8,128)S(1)} %collective-permute-done.3.refs_4_), channel_id=1, source_target_pairs={{0,4},{4,0},{1,5},{5,1},{2,6},{6,2},{3,7},{7,3},{8,12},{12,8},{9,1... | collective-permute-start | bytes 1843208 | tf_op jit(solution)/shard_map/ppermute | solution.py:18
  44.5 0.9 copy-start.3
  45.3 0.8 copy-start.4
  53.3 3.2 %copy-start = (bf16[3,20,256,256]{3,2,1,0:T(8,128)(2,1)S(1)}, bf16[3,20,256,256]{3,2,1,0:T(8,128)(2,1)}, u32[]{:S(2)}) copy-start(bf16[3,20,256,256]{3,2,1,0:T(8,128)(2,1)} %build_slabs.1) | copy-start | bytes 23592964
  67.8 36.9 %collective-permute-start.8 = (f32[128,2304]{1,0:T(8,128)S(1)}, f32[128,2304]{1,0:T(8,128)S(1)}, u32[]{:S(2)}, u32[]{:S(2)}) collective-permute-start(f32[128,2304]{1,0:T(8,128)S(1)} %contract_yz.5), channel_id=1, source_target_pairs={{0,16},{8,24},{16,0},{24,8},{1,17},{9,25},{17,1},{25,9},{2,18},{10... | collective-permute-start | bytes 3538952 | tf_op jit(solution)/shard_map/ppermute | solution.py:18
  79.6 28.9 %collective-permute-start.9 = (f32[128,2304]{1,0:T(8,128)S(1)}, f32[128,2304]{1,0:T(8,128)S(1)}, u32[]{:S(2)}, u32[]{:S(2)}) collective-permute-start(f32[128,2304]{1,0:T(8,128)S(1)} %contract_yz.6), channel_id=1, source_target_pairs={{0,24},{8,0},{16,8},{24,16},{1,25},{9,1},{17,9},{25,17},{2,26},{10... | collective-permute-start | bytes 3538952 | tf_op jit(solution)/shard_map/ppermute | solution.py:18
  92.5 41.5 %collective-permute-start.10 = (f32[128,2304]{1,0:T(8,128)S(1)}, f32[128,2304]{1,0:T(8,128)S(1)}, u32[]{:S(2)}, u32[]{:S(2)}) collective-permute-start(f32[128,2304]{1,0:T(8,128)S(1)} %contract_yz.7), channel_id=1, source_target_pairs={{0,8},{8,16},{16,24},{24,0},{1,9},{9,17},{17,25},{25,1},{2,10},{10... | collective-permute-start | bytes 3538952 | tf_op jit(solution)/shard_map/ppermute | solution.py:18
where the time goes:
time: 138 us
  Pallas kernels  56.1 us (41%)
  waiting for transfers between devices  53.9 us (39%)
  starting transfers between devices  12.8 us (9%)
  local copies, waits for them, and re-layouts  6.6 us (5%)
  matrix products  5.25 us (4%)
  other arithmetic  3.12 us (2%)
    ppermute x11, waiting for transfers between devices, shift(): lax.ppermute(array, axis, [(i, (i + step) % devices) for i in range(devic...  53.9 us
    pallas_call x4, Pallas kernels, contract(): pl.pallas_call(lambda *refs: contract_kernel(bx, *refs), in_specs=[pl.Blo...  45.1 us
    ppermute x11, starting transfers between devices, shift(): lax.ppermute(array, axis, [(i, (i + step) % devices) for i in range(devic...  12.8 us
    pallas_call x1, Pallas kernels, slabs(): pl.pallas_call(lambda *refs: slab_kernel(ny, *refs), grid=(STEPS,), in_sp...  7.08 us
    unnamed x18, local copies, waits for them, and re-layouts  4.08 us
    pallas_call x1, Pallas kernels, pack(): pl.pallas_call(pack_kernel, grid=(STEPS,), in_specs=[pl.BlockSpec((fold,...  3.99 us
    dot_general x4, matrix products, body(): term = jnp.dot(m, got[j], precision=HIGH)  3.79 us
  transfers between devices with their start and end apart: 11, of which 5 were waited for; matrix products, arithmetic and copies ran while one was open for 5% of the time, Pallas kernels for 27%

commit v1 on v0

v1 whole, which is shorter than its diff:
```python
import math

import jax
import jax.numpy as jnp
import numpy as np
from jax import lax
from jax.experimental import pallas as pl
from jax.experimental.pallas import tpu as pltpu
from jax.sharding import PartitionSpec as P

G = 48
BOX = 68
HALO = 34
LANES = 128
FOLD = LANES // HALO
BF = jnp.bfloat16
F32 = jnp.float32
MESH = pl.DeviceIdType.MESH
FAR = -1.0e6


def interp_values():
    offset = np.arange(G)[:, None] * BOX - np.arange(BOX)[None, :] * G
    summed = np.ones((G, BOX))
    for harmonic in range(1, G // 2):
        summed += 2.0 * np.cos(2.0 * math.pi / (G * BOX) * np.mod(harmonic * offset, G * BOX))
    return (summed / BOX).astype(np.float32)


def halves(value):
    high = value.astype(BF)
    return high, (value - high.astype(np.float32)).astype(BF)


def split(value):
    high = value.astype(BF)
    return high, (value - high.astype(F32)).astype(BF)


def octet_place(bx, i):
    c = i // 2
    odd = i % 2 == 1
    first = i < 2 * (HALO // 8)
    if isinstance(i, int):
        return (1, 8 * c) if odd else ((2, 8 * c) if first else (0, bx - HALO + 8 * (c - HALO // 8)))
    p = jnp.where(odd, 1, jnp.where(first, 2, 0))
    x0 = jnp.where(jnp.logical_or(odd, first), 8 * c, bx - HALO + 8 * (c - HALO // 8))
    return p, x0


def row_order(bx):
    octets = bx // 8 + 2 * (HALO // 8)
    rows = []
    for i in range(octets):
        p, x0 = octet_place(bx, i)
        rows += [(p, x0 + s) for s in range(8)]
    tail = [(0, x) for x in range(bx - HALO, bx)] + [(1, x) for x in range(bx)] + [(2, x) for x in range(HALO)]
    tail = [t for t in tail if t not in rows]
    assert len(tail) == 8 and len(set(rows + tail)) == len(rows) + 8
    return rows + tail, octets


def tables(bx, by, n, ny, slots):
    high, low = halves(interp_values())
    tab = np.zeros((2 * G, LANES), BF)
    tab[:G, :BOX], tab[G:, :BOX] = high, low
    tabt = np.zeros((LANES, 2 * LANES), BF)
    tabt[:BOX, :G], tabt[:BOX, LANES:LANES + G] = high.T, low.T
    tabi = np.zeros((2, G, slots, slots, LANES), BF)
    for f in range(slots):
        tabi[0, :, f, f, :BOX], tabi[1, :, f, f, :BOX] = high, low
    tabi = tabi.reshape(2 * G * slots, slots * LANES)
    rows, _ = row_order(bx)
    part = np.array([p for p, x in rows])
    ext = np.array([x - (bx - HALO) + (0, bx, 2 * bx)[p] for p, x in rows])
    cols = np.zeros((8, n * len(rows)), np.float32)
    cols[0] = np.tile(ext, n)
    cols[1] = np.tile(part - 1, n) - np.repeat(np.arange(n), len(rows))
    return tab, tabt, tabi, cols


def stages(bx, octets):
    step = 4 * FOLD
    ends = [min(step * (s + 1), bx) for s in range(-(-bx // step))]
    need = [octet_place(bx, i)[1] + 8 for i in range(octets)]
    plan, i = [], 0
    for s, end in enumerate(ends):
        start = i
        while i < octets and need[i] <= end:
            i += 1
        plan.append((step * s, end, start, i))
    return plan


def fused_kernel(info, pot, roots, tab, tabt, tabi, cols, got, mx, peer, pack, zin, zpeer, rt, yb, lhs, wz, us,
                 outb, raw_s, raw_r, z_s, z_r, rel_s, rel_r, rt_s, rt_r, gx_s, gx_r, own_s):
    n, ny, nz, slots = info
    bx, by, bz = pot.shape
    total_x, total_y, total_z = bx * n, by * ny, bz * nz
    rows, octets = row_order(bx)
    plan = stages(bx, octets)
    pad = yb.shape[1] // (2 * ny)
    half = ny * pad
    ix, iy, iz = lax.axis_index("gx"), lax.axis_index("gy"), lax.axis_index("gz")
    mate = {"gy": lax.rem(iy + 1, ny)}
    above = {"gz": lax.rem(iz + 1, nz)}
    below = {"gz": lax.rem(iz + nz - 1, nz)}
    holder = [{"gx": lax.rem(ix + n - j, n)} for j in range(n)]

    def copy(src, dst, ss, rs, where):
        return pltpu.make_async_remote_copy(
            src_ref=src, dst_ref=dst, send_sem=ss, recv_sem=rs, device_id=where, device_id_type=MESH)

    barrier = pltpu.get_barrier_semaphore()
    friends = [mate, above, below] + holder[1:]
    for where in friends:
        pl.semaphore_signal(barrier, inc=1, device_id=where, device_id_type=MESH)
    pl.semaphore_wait(barrier, len(friends))

    root_copy = [None] + [copy(roots, rt.at[j], rt_s.at[j], rt_r.at[j],
                               {"gx": lax.rem(ix + j, n)}) for j in range(1, n)]
    raw, zc, rel = [], [], []
    for s, (x0, x1, _, _) in enumerate(plan):
        xs = slice(x0, x1)
        rs = slice(x0 // FOLD, x1 // FOLD)
        raw.append(copy(pot.at[xs], peer.at[xs], raw_s.at[s], raw_r.at[s], mate))
        zc.append([copy(pack.at[side, rs], zin.at[side, rs], z_s.at[side, s], z_r.at[side, s], where)
                   for side, where in ((0, above), (1, below))])
        rel.append([copy(zin.at[side, rs], zpeer.at[side, rs], rel_s.at[side, s], rel_r.at[side, s], mate)
                    for side in (0, 1)])

    lane_p = lax.broadcasted_iota(jnp.int32, (by, LANES), 1)

    def pack_rows(x0, x1):
        def one(r, carry):
            down = jnp.zeros((by, LANES), F32)
            up = down
            for g in range(FOLD):
                v = pot[FOLD * r + g]
                mine = jnp.logical_and(lane_p >= g * HALO, lane_p < (g + 1) * HALO)
                down = jnp.where(mine, pltpu.roll(v, ((g + 1) * HALO) % LANES, 1), down)
                up = jnp.where(mine, pltpu.roll(v, g * HALO, 1) if g else v, up)
            pack[0, r] = down
            pack[1, r] = up
            return carry
        lax.fori_loop(x0 // FOLD, x1 // FOLD, one, 0)

    last = len(plan) - 1
    for s, (x0, x1, _, _) in enumerate(plan):
        pack_rows(x0, x1)
        raw[s].start()
        if s:
            for c in zc[s - 1]:
                c.start()
    for j in range(1, n):
        root_copy[j].start()
    for c in zc[last]:
        c.start()

    lane_r = lax.broadcasted_iota(jnp.int32, (1, LANES), 1)
    fix, fiy, fiz = ix.astype(F32), iy.astype(F32), iz.astype(F32)

    def wrapped(v, period):
        v = jnp.where(v < 0, v + period, v)
        return jnp.where(v >= period, v - period, v)

    def lane_sum(v):
        return jnp.sum(v, axis=1, keepdims=True)

    ye = lax.broadcasted_iota(jnp.int32, (1, half), 1)
    block_y = jnp.zeros((1, half), jnp.int32)
    for c in range(1, ny):
        block_y = block_y + (ye >= c * pad).astype(jnp.int32)
    real_y = ye - block_y * pad < by
    cells_y = jnp.where(real_y, (ye - block_y * (pad - by)).astype(F32), FAR)
    ze = lax.broadcasted_iota(jnp.int32, (2 * LANES, 1), 0)
    zf = ze.astype(F32)
    cells_z = jnp.where(ze < bz + HALO, zf + HALO, jnp.where(ze < bz + 2 * HALO, zf - (bz + HALO), FAR))
    sub_x = lax.broadcasted_iota(jnp.int32, (LANES, half), 0).astype(F32)
    lane_x = lax.broadcasted_iota(jnp.int32, (2 * LANES, LANES), 1).astype(F32)
    dot = lambda a, b: jnp.dot(a, b, preferred_element_type=F32)

    def matrices(j, source):
        rx, ry, rz = source[0:1, :], source[1:2, :], source[2:3, :]
        xm = wrapped(rx + HALO, total_x)
        ys = wrapped(ry - fiy * by, total_y)
        zs = wrapped(rz + HALO - fiz * bz, total_z)
        for p in range(3):
            target = wrapped(fix + (1 - p), n) * bx
            hit = jnp.logical_and(lane_r < slots, jnp.logical_and(xm >= target, xm < target + bx))
            some = lane_sum(jnp.where(hit, 1.0, 0.0)) > 0.5
            sy = lane_sum(jnp.where(hit, ys, 0.0))
            sz = lane_sum(jnp.where(hit, zs, 0.0))
            place = jnp.where(some, cells_y - sy, FAR)
            place = jnp.where(jnp.logical_and(place < 0, place > FAR / 2), place + total_y, place)
            hot = jnp.where(sub_x == place, 1.0, 0.0).astype(BF)
            m = dot(tab[...], hot).astype(BF)
            lhs[p, j * G:(j + 1) * G, :half] = m[:G]
            lhs[p, j * G:(j + 1) * G, half:2 * half] = m[:G]
            lhs[p, j * G:(j + 1) * G, 2 * half:] = m[G:]
            place = jnp.where(some, cells_z - sz, FAR)
            hot = jnp.where(lane_x == place, 1.0, 0.0).astype(BF)
            wz[j, p] = dot(hot, tabt[...]).astype(BF)

    matrices(0, roots)
    xm = wrapped(roots[0:1, :] + HALO, total_x)
    hots = []
    sub_w = lax.broadcasted_iota(jnp.int32, (LANES, n * len(rows)), 0).astype(F32)
    ext, src = cols[0:1, :], cols[1:2, :]
    for f in range(slots):
        mine = lane_sum(jnp.where(lane_r == f, xm, 0.0))
        slab = jnp.zeros((1, 1), F32)
        for k in range(1, n):
            slab = slab + jnp.where(mine >= k * bx, 1.0, 0.0)
        t = src + (slab - fix)
        good = jnp.logical_or(t == 0, jnp.logical_or(t == n, t == -n))
        place = jnp.where(good, ext - (mine - slab * bx), FAR)
        hots.append(jnp.where(sub_w == place, 1.0, 0.0).astype(BF))
    mx[...] = dot(tabi[...], jnp.concatenate(hots, axis=0)).astype(BF)
    for j in range(1, n):
        root_copy[j].wait_recv()
        matrices(j, rt.at[j])

    lane_h = lax.broadcasted_iota(jnp.int32, (pad, LANES), 1)
    blank = jnp.zeros((pad - by, LANES), F32)

    def full(v):
        return jnp.concatenate([v, blank], axis=0)

    def slab_rows(x0, x1):
        def one(r, carry):
            for c, (block, halos) in enumerate(((pot, zin), (peer, zpeer))):
                down = full(halos[0, r])
                up = full(halos[1, r])
                for g in range(FOLD):
                    x = FOLD * r + g
                    a = pltpu.roll(up, (-g * HALO) % LANES, 1) if g else up
                    b = pltpu.roll(down, (HALO - g * HALO) % LANES, 1) if g != 1 else down
                    second = jnp.where(lane_h < HALO, a, jnp.where(lane_h < 2 * HALO, b, 0.0))
                    for side, v in ((0, full(block[x])), (1, second)):
                        h, l = split(v)
                        lanes = slice(side * LANES, (side + 1) * LANES)
                        yb[x, c * pad:(c + 1) * pad, lanes] = h
                        yb[x, half + c * pad:half + (c + 1) * pad, lanes] = l
            return carry
        lax.fori_loop(x0 // FOLD, x1 // FOLD, one, 0)

    def row(p, x, s):
        r = dot(lhs[p, :, :2 * half], yb[x]) + dot(lhs[p, :, 2 * half:], yb[x, :half])
        us[:, s, :] = r

    def finish(j, p):
        h, l = split(us[j * G:(j + 1) * G].reshape(G * 8, us.shape[2]))
        a = dot(h, wz[j, p])
        return a[:, :LANES] + a[:, LANES:] + dot(l, wz[j, p, :, :LANES])

    def store(j, i, r):
        at = pl.multiple_of(8 * i, 8)
        for b in range(G):
            outb[j, pl.ds(at, 8), b * G:(b + 1) * G] = r[8 * b:8 * b + 8, :G]

    def sent(j, i):
        at = pl.ds(pl.multiple_of(8 * i, 8), 8)
        return copy(outb.at[j, at], got.at[j, at], gx_s.at[j, i], gx_r.at[j, i], holder[j])

    def emit(i, value):
        previous = None
        for j in list(range(1, n)) + [0]:
            store(j, i, value(j))
            if previous:
                sent(previous, i).start()
            previous = j

    def octet(i, carry):
        p, x0 = octet_place(bx, i)
        for s in range(8):
            row(p, x0 + s, s)
        emit(i, lambda j: finish(j, p))
        return carry

    for c in zc[0]:
        c.wait_recv()
    for c in rel[0]:
        c.start()
    for s, (x0, x1, i0, i1) in enumerate(plan):
        raw[s].wait_recv()
        for c in rel[s]:
            c.wait_recv()
        slab_rows(x0, x1)
        lax.fori_loop(i0, i1 - 1, octet, 0)
        if s < last:
            for c in zc[s + 1]:
                c.wait_recv()
            for c in rel[s + 1]:
                c.start()
        octet(i1 - 1, 0)

    tail = rows[8 * octets:]
    for s, (p, x) in enumerate(tail):
        row(p, x, s)
    sub = lax.broadcasted_iota(jnp.int32, (G * 8, LANES), 0) % 8

    def tail_value(j):
        total = jnp.zeros((G * 8, LANES), F32)
        for p in range(3):
            places = [s for s, t in enumerate(tail) if t[0] == p]
            mine = jnp.logical_and(sub >= places[0], sub <= places[-1])
            total = jnp.where(mine, finish(j, p), total)
        return total

    emit(octets, tail_value)
    own = pltpu.make_async_copy(outb.at[0], got.at[0], own_s)
    own.start()
    for s in range(last + 1):
        raw[s].wait_send()
        for c in zc[s] + rel[s]:
            c.wait_send()
    for j in range(1, n):
        root_copy[j].wait_send()

    def finished(i, carry):
        for j in range(1, n):
            sent(j, i).wait()
        return carry

    lax.fori_loop(0, octets + 1, finished, 0)
    own.wait()


def fused(info, pot, roots, consts):
    n, ny, nz, slots = info
    bx, by, bz = pot.shape
    rows, octets = row_order(bx)
    count = len(rows)
    chunks = len(stages(bx, octets))
    pad = -(-by // 16) * 16
    half = ny * pad
    dma = pltpu.SemaphoreType.DMA
    vmem = pl.BlockSpec(memory_space=pltpu.VMEM)
    folded = (2, bx // FOLD, by, LANES)
    return pl.pallas_call(
        lambda *refs: fused_kernel(info, *refs),
        in_specs=[vmem] * 6,
        out_specs=[pl.BlockSpec(memory_space=pl.ANY), vmem],
        out_shape=[jax.ShapeDtypeStruct((n, count, G * G), F32),
                   jax.ShapeDtypeStruct((2 * G * slots, n * count), BF)],
        scratch_shapes=[
            pltpu.VMEM((bx, by, LANES), F32),
            pltpu.VMEM(folded, F32),
            pltpu.VMEM(folded, F32),
            pltpu.VMEM(folded, F32),
            pltpu.VMEM((n, 8, LANES), F32),
            pltpu.VMEM((bx, 2 * half, 2 * LANES), BF),
            pltpu.VMEM((3, n * G, 3 * half), BF),
            pltpu.VMEM((n, 3, 2 * LANES, 2 * LANES), BF),
            pltpu.VMEM((n * G, 8, 2 * LANES), F32),
            pltpu.VMEM((n, count, G * G), F32),
            dma((chunks,)), dma((chunks,)),
            dma((2, chunks)), dma((2, chunks)),
            dma((2, chunks)), dma((2, chunks)),
            dma((n,)), dma((n,)),
            dma((n, octets + 1)), dma((n, octets + 1)),
            dma,
        ],
        compiler_params=pltpu.CompilerParams(
            collective_id=0, has_side_effects=True, vmem_limit_bytes=60 * 1024 * 1024),
        cost_estimate=pl.CostEstimate(flops=24 * 10 ** 9, bytes_accessed=16 * 1024 * 1024, transcendentals=0),
        name="exchange_contract",
    )(pot, roots, *consts)


def last_kernel(n, slots, mx, got, out):
    t = pl.program_id(0)
    count, width = got.shape[1], got.shape[2]
    m = G * slots
    dot = lambda a, b: jnp.dot(a, b, preferred_element_type=F32)
    total = None
    for j in range(n):
        h, l = split(got[j])
        both = mx[:, j * count:(j + 1) * count]
        a = dot(both, h)
        term = a[:m] + a[m:] + dot(both[:m], l)
        total = term if total is None else total + term
    for a in range(G):
        at = pl.multiple_of(a * G * G + t * width, LANES)
        out[:, pl.ds(at, width)] = total[a * slots:(a + 1) * slots]


def last(info, mx, got):
    n, ny, nz, slots = info
    count = got.shape[1]
    width = 2 * LANES
    return pl.pallas_call(
        lambda *refs: last_kernel(n, slots, *refs),
        grid=(G * G // width,),
        in_specs=[pl.BlockSpec(mx.shape, lambda t: (0, 0)),
                  pl.BlockSpec((n, count, width), lambda t: (0, 0, t))],
        out_specs=pl.BlockSpec((slots, G ** 3), lambda t: (0, 0)),
        out_shape=jax.ShapeDtypeStruct((slots, G ** 3), F32),
        compiler_params=pltpu.CompilerParams(vmem_limit_bytes=60 * 1024 * 1024),
        name="contract_x",
    )(mx, got)


def body(potential, frag_root):
    bx, by, bz = potential.shape
    n, ny, nz = lax.axis_size("gx"), lax.axis_size("gy"), lax.axis_size("gz")
    slots = frag_root.shape[1]
    info = (n, ny, nz, slots)
    roots = jnp.pad(frag_root.astype(F32), ((0, 5), (0, LANES - slots)))
    consts = [jnp.asarray(c) for c in tables(bx, by, n, ny, slots)]
    got, mx = fused(info, potential, roots, consts)
    return last(info, mx, got)


def solution(mesh):
    return jax.shard_map(
        body,
        mesh=mesh,
        in_specs=(P("gx", "gy", "gz"), P(None, ("gx", "gy", "gz"))),
        out_specs=P(("gx", "gy", "gz"), None),
        check_vma=False,
    )
```

time: 138 us -> 83.7 us (0.61)
  waiting for transfers between devices: 53.9 us -> 0 us
  Pallas kernels: 56.1 us -> 82.2 us
  starting transfers between devices: 12.8 us -> 0 us
  local copies, waits for them, and re-layouts: 6.6 us -> 0.6 us
  matrix products: 5.25 us -> 0 us
  other arithmetic: 3.12 us -> 0.68 us
    ppermute x11 -> x0, waiting for transfers between devices: 53.9 us -> none  [shift(): lax.ppermute(array, axis, [(i, (i + step) % devices) for i in range(devic...]
    pallas_call x6 -> x2, Pallas kernels: 56.1 us -> 82.2 us  [the longest x1 73.2 us: fused(): pl.pallas_call(lambda *refs: fused_kernel(info, *refs), in_specs=[vmem] *...]
    ppermute x11 -> x0, starting transfers between devices: 12.8 us -> none  [shift(): lax.ppermute(array, axis, [(i, (i + step) % devices) for i in range(devic...]
    dot_general x7 -> x0, matrix products: 5.25 us -> none  [the longest x4 3.79 us: body(): term = jnp.dot(m, got[j], precision=HIGH)]
    unnamed x18 -> x0, local copies, waits for them, and re-layouts: 4.08 us -> none
    div x1 -> x0, other arithmetic: 2.21 us -> none  [interp_values(): return summed / BOX]
    reshape x1 -> x0, local copies, waits for them, and re-layouts: 2.09 us -> none  [body(): return fields.reshape(slots, -1)]
  transfers between devices with their start and end apart: 11 -> 0, of which waited for: 5 -> 0; matrix products, arithmetic and copies ran while one was open for 5% -> 0% of each run, Pallas kernels for 27% -> 0%
where the time goes in v1:
time: 83.7 us; the launch traced here: 83.4 us
  Pallas kernels  82.2 us (98%)
    pallas_call x1, Pallas kernels, fused(): pl.pallas_call(lambda *refs: fused_kernel(info, *refs), in_specs=[vmem] *...  73.2 us
    pallas_call x1, Pallas kernels, last(): pl.pallas_call(lambda *refs: last_kernel(n, slots, *refs), grid=(G * G //...  8.94 us

profile of v1, /device:TPU:0, one launch (start us, length us, event | category | flops | bytes accessed | tf_op | source)
XLA Modules:
  0.0 83.4 jit_solution(6507602513660745698)
XLA Ops:
  0.0 0.7 convert_element_type.5
  0.7 0.6 pad.4.refs_1_
  1.3 73.2 %exchange_contract.1 = (f32[4,128,2304]{2,1,0:T(8,128)}, bf16[384,512]{1,0:T(8,128)(2,1)}) custom-call(f32[60,60,128]{2,1,0:T(8,128)} %refs_0_.1, f32[8,128]{1,0:T(8,128)} %pad.4.refs_1_, bf16[96,128]{1,0:T(8,128)(2,1)} %constant.11.clone.refs_2_, bf16[128,256]{1,0:T(8,128)(2,1)} %constant.12.clone.refs_3_, bf16[384,512]{1,0:T(8,128)(2,1)} %constant.13.clone.refs_4_, ...), custom_call_target="tpu_custom_call" | custom-call | flops 24000000000 | bytes 16777216 | tf_op jit(solution)/shard_map/exchange_contract/pallas_call | solution.py:341
  74.5 8.9 %contract_x.1 = f32[4,110592]{1,0:T(4,128)} custom-call(bf16[384,512]{1,0:T(8,128)(2,1)} %get-tuple-element.7.refs_0_, f32[4,128,2304]{2,1,0:T(8,128)} %get-tuple-element.8.refs_1_), custom_call_target="tpu_custom_call" | custom-call | tf_op jit(solution)/shard_map/contract_x/pallas_call | solution.py:393

commit v2 on v0

--- a/solution.py
+++ b/solution.py
@@ -2,6 +2,7 @@
 
 import jax
 import jax.numpy as jnp
+import numpy as np
 from jax import lax
 from jax.experimental import pallas as pl
 from jax.experimental.pallas import tpu as pltpu
@@ -10,7 +11,33 @@
 G = 48
 BOX = 68
 HALO = 34
+LANES = 128
+FOLD = LANES // HALO
+BF = jnp.bfloat16
+F32 = jnp.float32
+MESH = pl.DeviceIdType.MESH
+FAR = -1.0e6
+FAR_CELL = -(1 << 20)
+STEPS = 4
 HIGH = lax.Precision.HIGH
+
+
+def interp_values():
+    offset = np.arange(G)[:, None] * BOX - np.arange(BOX)[None, :] * G
+    summed = np.ones((G, BOX))
+    for harmonic in range(1, G // 2):
+        summed += 2.0 * np.cos(2.0 * math.pi / (G * BOX) * np.mod(harmonic * offset, G * BOX))
+    return (summed / BOX).astype(np.float32)
+
+
+def halves(value):
+    high = value.astype(BF)
+    return high, (value - high.astype(np.float32)).astype(BF)
+
+
+def split(value):
+    high = value.astype(BF)
+    return high, (value - high.astype(F32)).astype(BF)
 
 
 def shift(array, axis, step):
@@ -24,35 +51,10 @@
         place = jnp.mod(place, period)
     inside = jnp.logical_and(place >= 0, place < BOX)
     inside = jnp.logical_and(inside, valid[..., None])
-    base = interp_values()
+    base = jnp.asarray(interp_values())
     index = jnp.where(inside, place, BOX)
     hot = (index[..., None, :] == jnp.arange(BOX, dtype=jnp.int32)[:, None]).astype(jnp.float32)
     return jnp.einsum("ax,...xe->...ae", base, hot, precision=lax.Precision.HIGHEST)
-
-
-def interp_values():
-    row_index = jnp.arange(G, dtype=jnp.int32)[:, None]
-    col_index = jnp.arange(BOX, dtype=jnp.int32)[None, :]
-    offset = row_index * BOX - col_index * G
-    period = G * BOX
-    summed = jnp.ones((G, BOX), jnp.float32)
-    for harmonic in range(1, G // 2):
-        phase_angle = jnp.mod(harmonic * offset, period).astype(jnp.float32)
-        summed = summed + 2.0 * jnp.cos(2.0 * math.pi / period * phase_angle)
-    return summed / BOX
-
-
-LANES = 128
-FOLD = LANES // HALO
-STEPS = 4
-BF = jnp.bfloat16
-F32 = jnp.float32
-FAR = -(1 << 20)
-
-
-def split(value):
-    high = value.astype(BF)
-    return high, (value - high.astype(F32)).astype(BF)
 
 
 def pack_kernel(pot, low, high):
@@ -85,7 +87,7 @@
     )(pot)
 
 
-def slab_kernel(ny, *refs):
+def plain_slab_kernel(ny, *refs):
     owns, lows, highs, out = refs[:ny], refs[ny:2 * ny], refs[2 * ny:3 * ny], refs[3 * ny]
     rows, by = owns[0].shape[1], owns[0].shape[2]
     pad = out.shape[2] // (2 * ny)
@@ -120,7 +122,7 @@
     big = pl.BlockSpec((fold, step, by, LANES), lambda i: (0, i, 0, 0))
     small = pl.BlockSpec((step, by, LANES), lambda i: (i, 0, 0))
     return pl.pallas_call(
-        lambda *refs: slab_kernel(ny, *refs),
+        lambda *refs: plain_slab_kernel(ny, *refs),
         grid=(STEPS,),
         in_specs=[big] * ny + [small] * (2 * ny),
         out_specs=pl.BlockSpec((fold, step, 2 * ny * pad, 2 * LANES), lambda i: (0, i, 0, 0)),
@@ -166,7 +168,7 @@
 
     blocks = 2 * nl + nm
     lax.fori_loop(0, blocks, block, 0)
-    tail = tail_rows(bx)
+    tail = plain_tail_rows(bx)
     for s, (p, x) in enumerate(tail):
         row(p, x, s)
     sub = lax.broadcasted_iota(jnp.int32, (G * 8, G), 0) % 8
@@ -178,7 +180,7 @@
     store(total, 8 * blocks)
 
 
-def tail_rows(bx):
+def plain_tail_rows(bx):
     nl, nm = HALO // 8 * 8, bx // 8 * 8
     rows = [(0, bx - HALO + x) for x in range(nl, HALO)]
     rows += [(1, x) for x in range(nm, bx)]
@@ -187,14 +189,14 @@
     return rows
 
 
-def row_order(bx):
+def plain_row_order(bx):
     nl, nm = HALO // 8 * 8, bx // 8 * 8
     rows = [(0, bx - HALO + x) for x in range(nl)] + [(1, x) for x in range(nm)]
-    return rows + [(2, x) for x in range(nl)] + tail_rows(bx)
+    return rows + [(2, x) for x in range(nl)] + plain_tail_rows(bx)
 
 
 def contract(bx, yb, my, mz):
-    rows = len(row_order(bx))
+    rows = len(plain_row_order(bx))
     k = my.shape[2]
     width = yb.shape[2]
     return pl.pallas_call(
@@ -214,7 +216,7 @@
     )(yb, my, mz)
 
 
-def body(potential, frag_root):
+def plain_body(potential, frag_root):
     bx, by, bz = potential.shape
     n = lax.axis_size("gx")
     ny = lax.axis_size("gy")
@@ -242,7 +244,7 @@
     cells_y = e // pad * by + e % pad
     real_y = e % pad < by
     e = jnp.arange(2 * LANES, dtype=jnp.int32)
-    cells_z = jnp.where(e < bz + HALO, e + HALO, jnp.where(e < bz + 2 * HALO, e - bz - HALO, FAR))
+    cells_z = jnp.where(e < bz + HALO, e + HALO, jnp.where(e < bz + 2 * HALO, e - bz - HALO, FAR_CELL))
     delta = jnp.array([1, 0, -1], jnp.int32)
     hit = anchor[:, None, :] == jnp.mod(ix + delta, n)[None, :, None]
     valid = jnp.any(hit, axis=2)
@@ -260,7 +262,7 @@
     mine = jnp.mod(frag_root[0] + HALO, total_x)
     slab = mine // bx
     rel = mine - slab * bx
-    rows = row_order(bx)
+    rows = plain_row_order(bx)
     part = jnp.array([p for p, x in rows], jnp.int32)
     ext = jnp.array([x - (bx - HALO) if p == 0 else x + HALO + (p - 1) * bx for p, x in rows], jnp.int32)
     mx = placed(rel, ext, None, jnp.ones((slots,), bool))
@@ -273,6 +275,496 @@
     return fields.reshape(slots, -1)
 
 
+def octet_place(bx, i):
+    c = i // 2
+    odd = i % 2 == 1
+    first = i < 2 * (HALO // 8)
+    if isinstance(i, int):
+        return (1, 8 * c) if odd else ((2, 8 * c) if first else (0, bx - HALO + 8 * (c - HALO // 8)))
+    p = jnp.where(odd, 1, jnp.where(first, 2, 0))
+    x0 = jnp.where(jnp.logical_or(odd, first), 8 * c, bx - HALO + 8 * (c - HALO // 8))
+    return p, x0
+
+
+def layout(bx):
+    octets = bx // 8 + 2 * (HALO // 8)
+    placed_rows = [(p, x0 + s) for p, x0 in (octet_place(bx, i) for i in range(octets)) for s in range(8)]
+    tail = [(0, x) for x in range(bx - HALO, bx)] + [(1, x) for x in range(bx)] + [(2, x) for x in range(HALO)]
+    tail = [t for t in tail if t not in placed_rows]
+    assert len(tail) == 8 and len(set(placed_rows + tail)) == len(placed_rows) + 8
+    sides = [t for i in range(0, octets + 1, 2) for t in placed_rows[8 * i:8 * i + 8] if t[0] != 1]
+    mids = [t for t in placed_rows if t[0] == 1]
+    assert len(sides) == SIDES and len(mids) + 8 == MIDS
+    return sides, mids, tail, octets
+
+
+SIDES = 2 * (HALO // 8) * 8
+MIDS = 64
+BLOCK = SIDES + 64
+CHUNKS = (3, 4, 3, 2, 2, 2)
+
+
+def tables(bx, n, slots):
+    high, low = halves(interp_values())
+    tab = np.zeros((2 * G, LANES), BF)
+    tab[:G, :BOX], tab[G:, :BOX] = high, low
+    tabt = np.zeros((LANES, 2 * LANES), BF)
+    tabt[:BOX, :G], tabt[:BOX, LANES:LANES + G] = high.T, low.T
+    tabi = np.zeros((2, G, slots, slots, LANES), BF)
+    for f in range(slots):
+        tabi[0, :, f, f, :BOX], tabi[1, :, f, f, :BOX] = high, low
+    tabi = tabi.reshape(2 * G * slots, slots * LANES)
+    sides, mids, tail, _ = layout(bx)
+    reach = lambda p, x: x - (bx - HALO) + (0, bx, 2 * bx)[p]
+    cols = np.full((8, 2 * n * 64), FAR, np.float32)
+    for j in range(n):
+        for half, rows in ((0, sides), (1, [t if t[0] != 1 else None for t in tail])):
+            for r, t in enumerate(rows):
+                if t:
+                    cols[0:2, half * n * 64 + j * 64 + r] = reach(*t), t[0] - 1
+        for half in (0, 1):
+            cols[2, half * n * 64 + j * 64:half * n * 64 + (j + 1) * 64] = j
+        for a in range(G):
+            cols[3, n * 64 + j * 64 + 8 + a] = a
+    for r, t in enumerate(mids + tail):
+        if t[0] == 1:
+            cols[4, r] = cols[4, MIDS + r] = reach(*t)
+    return tab, tabt, tabi, cols
+
+
+def stages(bx, octets):
+    need = [octet_place(bx, i)[1] + 8 for i in range(octets)]
+    plan, i, t = [], 0, 0
+    for count in CHUNKS:
+        start, end = i, t + count
+        x0, x1 = min(t * LANES // HALO, bx), min(end * LANES // HALO, bx)
+        while i < octets and need[i] <= x1:
+            i += 1
+        plan.append((x0, x1, start, i, t, end))
+        t = end
+    assert x1 == bx and t == tiles_of(bx) and i == octets
+    return plan
+
+
+def tiles_of(bx):
+    return -(-bx * HALO // LANES)
+
+
+def fused_kernel(info, pot_hbm, own_root, tab, tabt, tabi, cols, out, pot, got, mx, peer, pack, zin, zpeer, rt, yb,
+                 lhs, wz, us, outb, mids, ma, acc, load_s, raw_s, raw_r, z_s, z_r, rel_s, rel_r, rt_s, rt_r,
+                 gx_s, gx_r):
+    n, ny, nz, slots = info
+    bx, by, bz = pot.shape
+    total_x, total_y, total_z = bx * n, by * ny, bz * nz
+    side_rows, mid_rows, tail, octets = layout(bx)
+    plan = stages(bx, octets)
+    last = len(plan) - 1
+    pad = yb.shape[1] // (2 * ny)
+    half = ny * pad
+    ix, iy, iz = lax.axis_index("gx"), lax.axis_index("gy"), lax.axis_index("gz")
+    mate = {"gy": lax.rem(iy + 1, ny)}
+    above = {"gz": lax.rem(iz + 1, nz)}
+    below = {"gz": lax.rem(iz + nz - 1, nz)}
+    spot = [ix, ix + 1 - 2 * lax.rem(ix, 2), lax.rem(ix + 2, 4), 3 - ix]
+    other = [{"gx": d} for d in spot]
+    order = [3, 1, 2]
+    bank = [3, 0, 1, 2]
+
+    def copy(src, dst, ss, rs, where):
+        return pltpu.make_async_remote_copy(
+            src_ref=src, dst_ref=dst, send_sem=ss, recv_sem=rs, device_id=where, device_id_type=MESH)
+
+    load = pltpu.make_async_copy(pot_hbm, pot, load_s)
+    load.start()
+    barrier = pltpu.get_barrier_semaphore()
+    friends = [above, below, mate] + other[1:]
+    for where in friends:
+        pl.semaphore_signal(barrier, inc=1, device_id=where, device_id_type=MESH)
+
+    root_copy = [None] + [copy(rt.at[0], rt.at[j], rt_s.at[j], rt_r.at[j], other[j]) for j in range(1, n)]
+    raw, zc, rel = [], [], []
+    for s, (x0, x1, _, _, t0, t1) in enumerate(plan):
+        xs = slice(x0, x1)
+        rs = slice(t0, t1)
+        raw.append(copy(pot.at[xs], peer.at[xs], raw_s.at[s], raw_r.at[s], mate))
+        zc.append([copy(pack.at[side, rs], zin.at[side, rs], z_s.at[side, s], z_r.at[side, s], where)
+                   for side, where in ((0, above), (1, below))])
+        rel.append([copy(zin.at[side, rs], zpeer.at[side, rs], rel_s.at[side, s], rel_r.at[side, s], mate)
+                    for side in (0, 1)])
+
+    lane_p = lax.broadcasted_iota(jnp.int32, (by, LANES), 1)
+
+    def pack_tile(t, carry):
+        down = jnp.zeros((by, LANES), F32)
+        up = down
+        x0 = LANES * t // HALO
+        for k in range(-(-LANES // HALO) + 1):
+            x = jnp.minimum(x0 + k, bx - 1)
+            at = HALO * x - LANES * t
+            v = pot[x]
+            mine = jnp.logical_and(lane_p >= at, lane_p < at + HALO)
+            down = jnp.where(mine, pltpu.roll(v, lax.rem(at + HALO + LANES, LANES), 1), down)
+            up = jnp.where(mine, pltpu.roll(v, lax.rem(at + LANES, LANES), 1), up)
+        pack[0, t] = down
+        pack[1, t] = up
+        return carry
+
+    rt[0] = jnp.zeros(rt.shape[1:], F32)
+    rt[0, :3, :slots] = own_root[...].astype(F32)
+    load.wait()
+    lax.fori_loop(0, tiles_of(bx), pack_tile, 0)
+    pl.semaphore_wait(barrier, len(friends))
+    for s in range(last + 1):
+        for c in zc[s]:
+            c.start()
+        raw[s].start()
+        if s == 0:
+            for j in range(1, n):
+                root_copy[j].start()
+
+    lane_r = lax.broadcasted_iota(jnp.int32, (1, LANES), 1)
+    fiy, fiz = iy.astype(F32), iz.astype(F32)
+    fspot = [d.astype(F32) for d in spot]
+
+    def wrapped(v, period):
+        v = jnp.where(v < 0, v + period, v)
+        return jnp.where(v >= period, v - period, v)
+
+    def lane_sum(v):
+        return jnp.sum(v, axis=1, keepdims=True)
+
+    ye = lax.broadcasted_iota(jnp.int32, (1, half), 1)
+    block_y = jnp.zeros((1, half), jnp.int32)
+    for c in range(1, ny):
+        block_y = block_y + (ye >= c * pad).astype(jnp.int32)
+    real_y = ye - block_y * pad < by
+    cells_y = jnp.where(real_y, (ye - block_y * (pad - by)).astype(F32), FAR)
+    ze = lax.broadcasted_iota(jnp.int32, (2 * LANES, 1), 0)
+    zf = ze.astype(F32)
+    cells_z = jnp.where(ze < bz + HALO, zf + HALO, jnp.where(ze < bz + 2 * HALO, zf - (bz + HALO), FAR))
+    sub_x = lax.broadcasted_iota(jnp.int32, (LANES, LANES), 0).astype(F32)
+    lane_x = lax.broadcasted_iota(jnp.int32, (2 * LANES, LANES), 1).astype(F32)
+    dot = lambda a, b: jnp.dot(a, b, preferred_element_type=F32)
+
+    def matrices(j, source):
+        rx, ry, rz = source[0:1, :], source[1:2, :], source[2:3, :]
+        xm = wrapped(rx + HALO, total_x)
+        ys = wrapped(ry - fiy * by, total_y)
+        zs = wrapped(rz + HALO - fiz * bz, total_z)
+        for p in range(3):
+            target = wrapped(fspot[0] + (1 - p), n) * bx
+            hit = jnp.logical_and(lane_r < slots, jnp.logical_and(xm >= target, xm < target + bx))
+            some = lane_sum(jnp.where(hit, 1.0, 0.0)) > 0.5
+            sx = lane_sum(jnp.where(hit, xm, 0.0)) - target
+            sy = lane_sum(jnp.where(hit, ys, 0.0))
+            sz = lane_sum(jnp.where(hit, zs, 0.0))
+            place = jnp.where(some, cells_y - sy, FAR)
+            place = jnp.where(jnp.logical_and(place < 0, place > FAR / 2), place + total_y, place)
+            hot = jnp.where(sub_x == place, 1.0, 0.0).astype(BF)
+            m = dot(tab[...], hot).astype(BF)
+            lhs[p, bank[j] * G:(bank[j] + 1) * G, :half] = m[:G]
+            lhs[p, bank[j] * G:(bank[j] + 1) * G, half:2 * half] = m[:G]
+            lhs[p, bank[j] * G:(bank[j] + 1) * G, 2 * half:] = m[G:]
+            place = jnp.where(some, cells_z - sz, FAR)
+            hot = jnp.where(lane_x == place, 1.0, 0.0).astype(BF)
+            wz[j, p] = dot(hot, tabt[...]).astype(BF)
+            if p == 1:
+                place = jnp.where(some, cols[4:5, :LANES] - sx, FAR)
+                hot = jnp.where(sub_x == place, 1.0, 0.0).astype(BF)
+                m = dot(tab[...], hot).astype(BF)
+                ma[j, :, :LANES] = m[:G]
+                ma[j, :, LANES:] = m[G:]
+
+    for j in range(n):
+        outb[j, SIDES + 8 + G:] = jnp.zeros((BLOCK - SIDES - 8 - G, G * G), F32)
+        if j:
+            got[j, SIDES + 8 + G:] = jnp.zeros((BLOCK - SIDES - 8 - G, G * G), F32)
+    matrices(0, rt.at[0])
+    xm = wrapped(rt[0, 0:1, :] + HALO, total_x)
+    hots = []
+    wide = cols.shape[1]
+    sub_w = lax.broadcasted_iota(jnp.int32, (LANES, wide), 0).astype(F32)
+    ext, shifted, turn, inner = cols[0:1, :], cols[1:2, :], cols[2:3, :], cols[3:4, :]
+    srcs = jnp.zeros((1, wide), F32)
+    for j in range(n):
+        srcs = jnp.where(turn == j, fspot[j], srcs)
+    high_rows = G * slots
+    line = lax.broadcasted_iota(jnp.int32, (high_rows, 1), 0)
+    line_f = lax.rem(line, slots)
+    line_a = (line - line_f).astype(F32) * (1.0 / slots)
+    slab_of = jnp.zeros((high_rows, 1), F32)
+    for f in range(slots):
+        mine = lane_sum(jnp.where(lane_r == f, xm, 0.0))
+        slab = jnp.zeros((1, 1), F32)
+        for k in range(1, n):
+            slab = slab + jnp.where(mine >= k * bx, 1.0, 0.0)
+        t = shifted + (slab - srcs)
+        good = jnp.logical_or(t == 0, jnp.logical_or(t == n, t == -n))
+        place = jnp.where(good, ext - (mine - slab * bx), FAR)
+        hots.append(jnp.where(sub_w == place, 1.0, 0.0).astype(BF))
+        slab_of = jnp.where(line_f == f, slab, slab_of)
+    m = dot(tabi[...], jnp.concatenate(hots, axis=0))
+    same = jnp.logical_and(line_a == inner, slab_of == srcs)
+    mx[:high_rows] = jnp.where(same, 1.0, m[:high_rows]).astype(BF)
+    mx[high_rows:] = m[high_rows:].astype(BF)
+    for j in range(1, n):
+        root_copy[j].wait_recv()
+        matrices(j, rt.at[j])
+
+    lane_h = lax.broadcasted_iota(jnp.int32, (pad, LANES), 1)
+    blank = jnp.zeros((pad - by, LANES), F32)
+
+    def full(v):
+        return jnp.concatenate([v, blank], axis=0)
+
+    def keep(x, c, side, v):
+        h, l = split(v)
+        lanes = slice(side * LANES, (side + 1) * LANES)
+        yb[x, c * pad:(c + 1) * pad, lanes] = h
+        yb[x, half + c * pad:half + (c + 1) * pad, lanes] = l
+
+    def inner_row(c, block):
+        def one(x, carry):
+            keep(x, c, 0, full(block[x]))
+            return carry
+        return one
+
+    def halo_row(x, carry):
+        t = HALO * x // LANES
+        at = HALO * x - LANES * t
+        t_next = (HALO * x + HALO - 1) // LANES
+        back = lax.rem(LANES - at, LANES)
+        for c, halos in enumerate((zin, zpeer)):
+            def piece(side, place):
+                turn = lax.rem(back + place, LANES)
+                one = pltpu.roll(full(halos[side, t]), turn, 1)
+                two = pltpu.roll(full(halos[side, t_next]), turn, 1)
+                return jnp.where(lane_h - place < LANES - at, one, two)
+            second = jnp.where(lane_h < HALO, piece(1, 0), jnp.where(lane_h < 2 * HALO, piece(0, HALO), 0.0))
+            keep(x, c, 1, second)
+        return carry
+
+    def row(p, x, s, group):
+        first, count = (bank[0] * G, G) if group == [0] else (0, (n - 1) * G)
+        m = slice(first, first + count)
+        r = dot(lhs[p, m, :2 * half], yb[x]) + dot(lhs[p, m, 2 * half:], yb[x, :half])
+        for side in range(2):
+            us[side, pl.ds(first * 8 + s, count, stride=8), :] = r[:, side * LANES:(side + 1) * LANES]
+
+    def finish(j, p):
+        held = slice(bank[j] * G * 8, (bank[j] + 1) * G * 8)
+        h, l = split(jnp.concatenate([us[0, held], us[1, held]], axis=1))
+        a = dot(h, wz[j, p])
+        return a[:, :LANES] + a[:, LANES:] + dot(l, wz[j, p, :, :LANES])
+
+    def store(ref, j, at, r):
+        for b in range(G):
+            ref[j, pl.ds(at, 8), b * G:(b + 1) * G] = r[8 * b:8 * b + 8, :G]
+
+    def sent(j, q):
+        at = pl.ds(pl.multiple_of(8 * q, 8), 8)
+        return copy(outb.at[j, at], got.at[j, at], gx_s.at[j, q], gx_r.at[j, q], other[j])
+
+    def sent_mid(j):
+        at = pl.ds(SIDES + 8, G)
+        q = SIDES // 8 + 1
+        return copy(outb.at[j, at], got.at[j, at], gx_s.at[j, q], gx_r.at[j, q], other[j])
+
+    def emit(work, send, group):
+        previous = None
+        for j in group:
+            work(j)
+            if previous:
+                send(previous).start()
+            previous = j
+
+    def side_octet(group, c0):
+        def one(c, carry):
+            p, x0 = octet_place(bx, 2 * c)
+            for s in range(8):
+                row(p, x0 + s, s, group)
+            if group[-1]:
+                @pl.when(c > c0)
+                def _():
+                    sent(group[-1], c - 1).start()
+            emit(lambda j: store(outb, j, pl.multiple_of(8 * c, 8), finish(j, p)), lambda j: sent(j, c), group)
+            return carry
+        return one
+
+    def mid_octet(group):
+        def one(c, carry):
+            for s in range(8):
+                row(1, 8 * c + s, s, group)
+            for j in group:
+                store(mids, j, pl.multiple_of(8 * c, 8), finish(j, 1))
+            return carry
+        return one
+
+    def tail_octet(group):
+        for k, (p, x) in enumerate(tail):
+            row(p, x, k, group)
+        if group[-1]:
+            sent(group[-1], SIDES // 8 - 1).start()
+        sub = lax.broadcasted_iota(jnp.int32, (G * 8, LANES), 0) % 8
+
+        def work(j):
+            total = jnp.zeros((G * 8, LANES), F32)
+            for p in range(3):
+                places = [k for k, t in enumerate(tail) if t[0] == p]
+                mine = jnp.logical_and(sub >= places[0], sub <= places[-1])
+                total = jnp.where(mine, finish(j, p), total)
+            store(outb, j, SIDES, total)
+            store(mids, j, MIDS - 8, total)
+
+        emit(work, lambda j: sent(j, SIDES // 8), group)
+
+    lax.fori_loop(0, bx, inner_row(0, pot), 0)
+    for c in raw:
+        c.wait_recv()
+    lax.fori_loop(0, bx, inner_row(1, peer), 0)
+    for c in zc[0]:
+        c.wait_recv()
+    for c in rel[0]:
+        c.start()
+    for s, (x0, x1, i0, i1, _, _) in enumerate(plan):
+        for c in rel[s]:
+            c.wait_recv()
+        lax.fori_loop(x0, x1, halo_row, 0)
+        c0, c1 = (i0 + 1) // 2, (i1 + 1) // 2
+        lax.fori_loop(c0, c1, side_octet(order, c0), 0)
+        if s < last:
+            for c in zc[s + 1]:
+                c.wait_recv()
+            for c in rel[s + 1]:
+                c.start()
+            if c1 > c0:
+                sent(order[-1], c1 - 1).start()
+        else:
+            tail_octet(order)
+        lax.fori_loop(i0 // 2, i1 // 2, mid_octet(order), 0)
+
+    tile = 2 * LANES
+    tiles = G * G // tile
+
+    def mid_work(j):
+        def one(t, carry):
+            at = pl.ds(pl.multiple_of(t * tile, tile), tile)
+            h, l = split(mids[j, :, at])
+            both = jnp.concatenate([h, l], axis=0)
+            outb[j, SIDES + 8:SIDES + 8 + G, at] = (
+                dot(ma[j, :, :2 * MIDS], both) + dot(ma[j, :, LANES:LANES + MIDS], h))
+            return carry
+        lax.fori_loop(0, tiles, one, 0)
+
+    sent(order[-1], SIDES // 8).start()
+    emit(mid_work, sent_mid, order)
+    for s in range(8):
+        row(2, s, s, [0])
+    sent_mid(order[-1]).start()
+    lax.fori_loop(0, SIDES // 8, side_octet([0], 0), 0)
+    lax.fori_loop(0, octets // 2, mid_octet([0]), 0)
+    tail_octet([0])
+    mid_work(0)
+
+    def gather_rows(first, rows, at):
+        return jnp.concatenate([outb[0, first:first + rows, at]] + [got[j, first:first + rows, at]
+                                                                    for j in range(1, n)], axis=0)
+
+    def across(first, rows, k0, at):
+        h, l = split(gather_rows(first, rows, at))
+        both = dot(mx[:, k0:k0 + n * 64], h)
+        return both[:high_rows] + both[high_rows:] + dot(mx[:high_rows, k0:k0 + n * 64], l)
+
+    for s in range(last + 1):
+        raw[s].wait_send()
+        for c in zc[s] + rel[s]:
+            c.wait_send()
+    for j in range(1, n):
+        root_copy[j].wait_send()
+
+    def arrived(q, carry):
+        for j in range(1, n):
+            sent(j, q).wait()
+        return carry
+
+    lax.fori_loop(0, SIDES // 8, arrived, 0)
+
+    def first_part(t, carry):
+        at = pl.ds(pl.multiple_of(t * tile, tile), tile)
+        acc[:, at] = across(0, SIDES, 0, at)
+        return carry
+
+    lax.fori_loop(0, tiles, first_part, 0)
+    arrived(SIDES // 8, 0)
+    for j in range(1, n):
+        sent_mid(j).wait()
+
+    def second_part(t, carry):
+        at = pl.ds(pl.multiple_of(t * tile, tile), tile)
+        r = acc[:, at] + across(SIDES, 64, n * 64, at)
+        for a in range(G):
+            where = pl.multiple_of(a * G * G + t * tile, LANES)
+            out[:, pl.ds(where, tile)] = r[a * slots:(a + 1) * slots]
+        return carry
+
+    lax.fori_loop(0, tiles, second_part, 0)
+
+
+def fused(info, pot, roots, consts):
+    n, ny, nz, slots = info
+    bx, by, bz = pot.shape
+    octets = layout(bx)[3]
+    chunks = len(CHUNKS)
+    pad = -(-by // 16) * 16
+    half = ny * pad
+    dma = pltpu.SemaphoreType.DMA
+    vmem = pl.BlockSpec(memory_space=pltpu.VMEM)
+    folded = (2, tiles_of(bx), by, LANES)
+    return pl.pallas_call(
+        lambda *refs: fused_kernel(info, *refs),
+        in_specs=[pl.BlockSpec(memory_space=pl.ANY)] + [vmem] * 5,
+        out_specs=vmem,
+        out_shape=jax.ShapeDtypeStruct((slots, G ** 3), F32),
+        scratch_shapes=[
+            pltpu.VMEM((bx, by, LANES), F32),
+            pltpu.VMEM((n, BLOCK, G * G), F32),
+            pltpu.VMEM((2 * G * slots, 2 * n * 64), BF),
+            pltpu.VMEM((bx, by, LANES), F32),
+            pltpu.VMEM(folded, F32),
+            pltpu.VMEM(folded, F32),
+            pltpu.VMEM(folded, F32),
+            pltpu.VMEM((n, 8, LANES), F32),
+            pltpu.VMEM((bx, 2 * half, 2 * LANES), BF),
+            pltpu.VMEM((3, n * G, 3 * half), BF),
+            pltpu.VMEM((n, 3, 2 * LANES, 2 * LANES), BF),
+            pltpu.VMEM((2, n * G * 8, LANES), F32),
+            pltpu.VMEM((n, BLOCK, G * G), F32),
+            pltpu.VMEM((n, MIDS, G * G), F32),
+            pltpu.VMEM((n, G, 2 * LANES), BF),
+            pltpu.VMEM((G * slots, G * G), F32),
+            dma, dma((chunks,)), dma((chunks,)),
+            dma((2, chunks)), dma((2, chunks)),
+            dma((2, chunks)), dma((2, chunks)),
+            dma((n,)), dma((n,)),
+            dma((n, SIDES // 8 + 2)), dma((n, SIDES // 8 + 2)),
+        ],
+        compiler_params=pltpu.CompilerParams(
+            collective_id=0, has_side_effects=True, vmem_limit_bytes=56 * 1024 * 1024),
+        cost_estimate=pl.CostEstimate(flops=24 * 10 ** 9, bytes_accessed=16 * 1024 * 1024, transcendentals=0),
+        name="exchange_contract",
+    )(pot, roots, *consts)
+
+
+def body(potential, frag_root):
+    bx, by, bz = potential.shape
+    n, ny, nz = lax.axis_size("gx"), lax.axis_size("gy"), lax.axis_size("gz")
+    slots = frag_root.shape[1]
+    if n != 4:
+        return plain_body(potential, frag_root)
+    consts = [jnp.asarray(c) for c in tables(bx, n, slots)]
+    return fused((n, ny, nz, slots), potential, frag_root, consts)
+
+
 def solution(mesh):
     return jax.shard_map(
         body,

time: 138 us -> 78.9 us (0.57)
  waiting for transfers between devices: 53.9 us -> 0 us
  Pallas kernels: 56.1 us -> 75.9 us
  starting transfers between devices: 12.8 us -> 0 us
  matrix products: 5.25 us -> 0 us
  local copies, waits for them, and re-layouts: 6.6 us -> 2.8 us
  other arithmetic: 3.12 us -> 0 us
    ppermute x11 -> x0, waiting for transfers between devices: 53.9 us -> none  [shift(): lax.ppermute(array, axis, [(i, (i + step) % devices) for i in range(devic...]
    pallas_call x6 -> x1, Pallas kernels: 56.1 us -> 75.9 us  [fused(): pl.pallas_call(lambda *refs: fused_kernel(info, *refs), in_specs=[pl.Bloc...]
    ppermute x11 -> x0, starting transfers between devices: 12.8 us -> none  [shift(): lax.ppermute(array, axis, [(i, (i + step) % devices) for i in range(devic...]
    dot_general x7 -> x0, matrix products: 5.25 us -> none  [the longest x4 3.79 us: body(): term = jnp.dot(m, got[j], precision=HIGH)]
    div x1 -> x0, other arithmetic: 2.21 us -> none  [interp_values(): return summed / BOX]
    reshape x1 -> x0, local copies, waits for them, and re-layouts: 2.09 us -> none  [body(): return fields.reshape(slots, -1)]
    unnamed x18 -> x1, local copies, waits for them, and re-layouts: 4.08 us -> 2.8 us
  transfers between devices with their start and end apart: 11 -> 0, of which waited for: 5 -> 0; matrix products, arithmetic and copies ran while one was open for 5% -> 0% of each run, Pallas kernels for 27% -> 0%
where the time goes in v2:
time: 78.9 us; the launch traced here: 78.7 us
  Pallas kernels  75.9 us (96%)
  local copies, waits for them, and re-layouts  2.8 us (4%)
    pallas_call x1, Pallas kernels, fused(): pl.pallas_call(lambda *refs: fused_kernel(info, *refs), in_specs=[pl.Bloc...  75.9 us
    unnamed x1, local copies, waits for them, and re-layouts  2.8 us

profile of v2, /device:TPU:0, one launch (start us, length us, event | category | flops | bytes accessed | tf_op | source)
XLA Modules:
  0.0 78.7 jit_solution(16208975651322928651)
XLA Ops:
  0.0 75.9 %exchange_contract.1 = f32[4,110592]{1,0:T(4,128)} custom-call(f32[60,60,128]{2,1,0:T(8,128)} %refs_0_.1, s32[3,4]{1,0:T(4,128)} %refs_1_.1, bf16[96,128]{1,0:T(8,128)(2,1)} %constant.8.clone.refs_2_, bf16[128,256]{1,0:T(8,128)(2,1)} %constant.9.clone.refs_3_, bf16[384,512]{1,0:T(8,128)(2,1)} %constant.10.clone.refs_4_, f32[8,512]{1,0:T(8,128)} %constant.11.clone.refs_5_), custom_call_target="tpu_custom_call" | custom-call | flops 24000000000 | bytes 16777216 | tf_op jit(solution)/shard_map/exchange_contract/pallas_call | solution.py:723
  75.9 2.8 %copy.8 = f32[4,110592]{1,0:T(4,128)} copy(f32[4,110592]{1,0:T(4,128)} %exchange_contract.1) | data formatting | bytes 3538944

commit v3 on v2

--- a/solution.py
+++ b/solution.py
@@ -301,7 +301,7 @@
 SIDES = 2 * (HALO // 8) * 8
 MIDS = 64
 BLOCK = SIDES + 64
-CHUNKS = (3, 4, 3, 2, 2, 2)
+CHUNKS = (3, 2, 2, 3, 2, 2, 2)
 
 
 def tables(bx, n, slots):
@@ -374,8 +374,11 @@
         return pltpu.make_async_remote_copy(
             src_ref=src, dst_ref=dst, send_sem=ss, recv_sem=rs, device_id=where, device_id_type=MESH)
 
-    load = pltpu.make_async_copy(pot_hbm, pot, load_s)
-    load.start()
+    lead = plan[0][1] + 1
+    loads = [pltpu.make_async_copy(pot_hbm.at[rows], pot.at[rows], load_s.at[k])
+             for k, rows in enumerate((slice(0, lead), slice(lead, bx)))]
+    for load in loads:
+        load.start()
     barrier = pltpu.get_barrier_semaphore()
     friends = [above, below, mate] + other[1:]
     for where in friends:
@@ -394,12 +397,12 @@
 
     lane_p = lax.broadcasted_iota(jnp.int32, (by, LANES), 1)
 
-    def pack_tile(t, carry):
+    def pack_tile(t, limit):
         down = jnp.zeros((by, LANES), F32)
         up = down
         x0 = LANES * t // HALO
         for k in range(-(-LANES // HALO) + 1):
-            x = jnp.minimum(x0 + k, bx - 1)
+            x = jnp.minimum(x0 + k, limit - 1)
             at = HALO * x - LANES * t
             v = pot[x]
             mine = jnp.logical_and(lane_p >= at, lane_p < at + HALO)
@@ -407,20 +410,31 @@
             up = jnp.where(mine, pltpu.roll(v, lax.rem(at + LANES, LANES), 1), up)
         pack[0, t] = down
         pack[1, t] = up
-        return carry
+
+    def pack_tiles(t0, t1, limit):
+        lax.fori_loop(t0, t1, lambda t, carry: (pack_tile(t, limit), carry)[1], 0)
 
     rt[0] = jnp.zeros(rt.shape[1:], F32)
     rt[0, :3, :slots] = own_root[...].astype(F32)
-    load.wait()
-    lax.fori_loop(0, tiles_of(bx), pack_tile, 0)
+    loads[0].wait()
+    pack_tiles(*plan[0][4:], lead)
+    loads[1].wait()
     pl.semaphore_wait(barrier, len(friends))
     for s in range(last + 1):
+        if 0 < s < last:
+            pack_tiles(*plan[s + 1][4:], bx)
         for c in zc[s]:
             c.start()
         raw[s].start()
         if s == 0:
             for j in range(1, n):
                 root_copy[j].start()
+            pack_tiles(*plan[1][4:], bx)
+        if s == last - 1:
+            for j in range(n):
+                outb[j, SIDES + 8 + G:] = jnp.zeros((BLOCK - SIDES - 8 - G, G * G), F32)
+                if j:
+                    got[j, SIDES + 8 + G:] = jnp.zeros((BLOCK - SIDES - 8 - G, G * G), F32)
 
     lane_r = lax.broadcasted_iota(jnp.int32, (1, LANES), 1)
     fiy, fiz = iy.astype(F32), iz.astype(F32)
@@ -475,10 +489,6 @@
                 ma[j, :, :LANES] = m[:G]
                 ma[j, :, LANES:] = m[G:]
 
-    for j in range(n):
-        outb[j, SIDES + 8 + G:] = jnp.zeros((BLOCK - SIDES - 8 - G, G * G), F32)
-        if j:
-            got[j, SIDES + 8 + G:] = jnp.zeros((BLOCK - SIDES - 8 - G, G * G), F32)
     matrices(0, rt.at[0])
     xm = wrapped(rt[0, 0:1, :] + HALO, total_x)
     hots = []
@@ -605,14 +615,18 @@
             row(p, x, k, group)
         if group[-1]:
             sent(group[-1], SIDES // 8 - 1).start()
-        sub = lax.broadcasted_iota(jnp.int32, (G * 8, LANES), 0) % 8
 
         def work(j):
-            total = jnp.zeros((G * 8, LANES), F32)
+            base = bank[j] * G * 8
             for p in range(3):
-                places = [k for k, t in enumerate(tail) if t[0] == p]
-                mine = jnp.logical_and(sub >= places[0], sub <= places[-1])
-                total = jnp.where(mine, finish(j, p), total)
+                spots = [pl.ds(base + k, G, stride=8) for k, t in enumerate(tail) if t[0] == p]
+                both = [jnp.concatenate([us[side, at] for at in spots], axis=0) for side in range(2)]
+                h, l = split(jnp.concatenate(both, axis=1))
+                a = dot(h, wz[j, p])
+                a = a[:, :LANES] + a[:, LANES:] + dot(l, wz[j, p, :, :LANES])
+                for k, at in enumerate(spots):
+                    us[0, at, :] = a[k * G:(k + 1) * G]
+            total = us[0, base:base + G * 8]
             store(outb, j, SIDES, total)
             store(mids, j, MIDS - 8, total)
 
@@ -742,7 +756,7 @@
             pltpu.VMEM((n, MIDS, G * G), F32),
             pltpu.VMEM((n, G, 2 * LANES), BF),
             pltpu.VMEM((G * slots, G * G), F32),
-            dma, dma((chunks,)), dma((chunks,)),
+            dma((2,)), dma((chunks,)), dma((chunks,)),
             dma((2, chunks)), dma((2, chunks)),
             dma((2, chunks)), dma((2, chunks)),
             dma((n,)), dma((n,)),

time: 78.9 us -> 75.4 us (0.956)
  Pallas kernels: 75.9 us -> 72.4 us
    pallas_call x1, Pallas kernels: 75.9 us -> 72.4 us  [fused(): pl.pallas_call(lambda *refs: fused_kernel(info, *refs), in_specs=[pl.Bloc...]
where the time goes in v3:
time: 75.4 us; the launch traced here: 75.2 us
  Pallas kernels  72.4 us (96%)
  local copies, waits for them, and re-layouts  2.8 us (4%)
    pallas_call x1, Pallas kernels, fused(): pl.pallas_call(lambda *refs: fused_kernel(info, *refs), in_specs=[pl.Bloc...  72.4 us
    unnamed x1, local copies, waits for them, and re-layouts  2.8 us

profile of v3, /device:TPU:0, one launch (start us, length us, event | category | flops | bytes accessed | tf_op | source)
XLA Modules:
  0.0 75.2 jit_solution(27478359562831371)
XLA Ops:
  0.0 72.4 %exchange_contract.1 = f32[4,110592]{1,0:T(4,128)} custom-call(f32[60,60,128]{2,1,0:T(8,128)} %refs_0_.1, s32[3,4]{1,0:T(4,128)} %refs_1_.1, bf16[96,128]{1,0:T(8,128)(2,1)} %constant.8.clone.refs_2_, bf16[128,256]{1,0:T(8,128)(2,1)} %constant.9.clone.refs_3_, bf16[384,512]{1,0:T(8,128)(2,1)} %constant.10.clone.refs_4_, f32[8,512]{1,0:T(8,128)} %constant.11.clone.refs_5_), custom_call_target="tpu_custom_call" | custom-call | flops 24000000000 | bytes 16777216 | tf_op jit(solution)/shard_map/exchange_contract/pallas_call | solution.py:737
  72.4 2.8 %copy.8 = f32[4,110592]{1,0:T(4,128)} copy(f32[4,110592]{1,0:T(4,128)} %exchange_contract.1) | data formatting | bytes 3538944
